TPU v7x, 32 devices: a whole 2x2x4 slice. The times are simulated.
32 devices in a mesh: row: 8 (over y, x, core), col: 4 (over z).
Axes of the slice: x: 2, y: 2, z: 4, core: 2. Of those that a mesh axis runs over, the one named last changes fastest.
Arguments:
- tokens: bfloat16 [1024, 8192], P('row', 'col'), may hold values from -6 to 6
- weights: bfloat16 [2, 14336, 8192], P(None, 'row', 'col'), may hold values from -0.0625 to 0.0625
- gradients: bfloat16 [2, 14336, 8192], P(None, 'row', 'col'), may hold values from -200 to 200, as said below
- row_factors: float32 [2, 14336], P(None, 'row'), may hold values from 0.05 to 0.5
- col_factors: float32 [2, 8192], P(None, 'col'), may hold values from 0.05 to 0.5
Outputs:
- hidden: bfloat16 [1024, 14336], P('col', 'row')
- row_new: float32 [2, 14336], P(None, 'row')
- col_new: float32 [2, 8192], P(None, 'col')
Inputs may be any that keep to these rules, and one draw needn't show every extreme that they name: Finite real gradients.
All inputs are finite; a program needn't handle non-finite values.
Results may differ from a plain program's by a relative error of at most 0.001.
The roundings to bfloat16 on the way count: a program that leaves them out, or rounds other values in their place, can miss the bound.
Values may be sent and summed in bfloat16 or wider, within the bound.
No kernel may reach another device: no remote copies, remote signals or barrier semaphores. Data moves between devices by JAX's collectives and lax.ppermute only.
A program may use at most 128 MiB of HBM per device.

v0:
```python
import jax
import jax.numpy as jnp
from jax import lax
from jax.sharding import PartitionSpec as P

D = 8192
FF = 14336
decay_rate = 0.5
learn_rate = 0.01
clip_limit = 1.0
tiny_eps = 1e-30


def local(tokens, weights, gradients, row_factors, col_factors):
    gradient = gradients.astype(jnp.float32)
    squares = gradient * gradient
    row_part = jnp.sum(squares, axis=2)
    col_part = jnp.sum(squares, axis=1)
    row_block = row_part.shape[1]
    col_block = col_part.shape[1]
    row_total = lax.psum(row_part, "col")
    col_total = lax.psum(col_part, "row")
    row_new = decay_rate * row_factors + (1.0 - decay_rate) * (row_total / D + tiny_eps)
    col_new = decay_rate * col_factors + (1.0 - decay_rate) * (col_total / FF + tiny_eps)
    row_mean = lax.psum(jnp.sum(row_new, axis=1), "row") / FF
    denominator = jnp.sqrt(row_new[:, :, None] * col_new[:, None, :] / row_mean[:, None, None])
    update = gradient / denominator
    norm_total = lax.psum(jnp.sum(update * update, axis=(1, 2)), ("row", "col"))
    clip_scale = jnp.maximum(1.0, jnp.sqrt(norm_total / (FF * D)) / clip_limit)
    new_weights = (
        weights.astype(jnp.float32) - learn_rate * update / clip_scale[:, None, None]
    ).astype(jnp.bfloat16)
    spread = lax.all_gather(tokens, "row", axis=0, tiled=True)
    flat_weights = new_weights.reshape(2 * row_block, col_block)
    combined = lax.psum_scatter(
        lax.dot_general(
            spread, flat_weights, (((1,), (1,)), ((), ())), preferred_element_type=jnp.float32
        ),
        "col",
        scatter_dimension=0,
        tiled=True,
    )
    gate_proj = combined[:, :row_block]
    up_proj = combined[:, row_block:]
    hidden = (jax.nn.silu(gate_proj) * up_proj).astype(jnp.bfloat16)
    return (hidden, row_new, col_new)


def solution(mesh):
    placed = (
        P("row", "col"),
        P(None, "row", "col"),
        P(None, "row", "col"),
        P(None, "row"),
        P(None, "col"),
    )
    return jax.shard_map(
        local,
        mesh=mesh,
        in_specs=placed,
        out_specs=(P("col", "row"), P(None, "row"), P(None, "col")),
        check_vma=False,
    )
```

profile of v0, /device:TPU:0, one launch (start us, length us, event | category | flops | bytes accessed | tf_op | source)
XLA Modules:
  0.0 409.2 jit_solution(4668442278646132492)
XLA Ops:
  7.2 0.0 copy-start.3
  7.2 0.0 copy-start.2
  7.2 0.0 all-gather.2.cloned.1.call-start
  7.2 9.1 %fusion = (f32[2,2048]{1,0:T(2,128)S(1)}, f32[2,1792]{1,0:T(2,128)S(1)}) fusion(bf16[2,1792,2048]{2,1,0:T(8,128)(2,1)} %param.7), kind=kLoop, calls=%fused_computation.2 | loop fusion | flops 29352448 | bytes 14710784 | tf_op jit(solution)/shard_map/reduce_sum | solution.py:18
  16.4 20.5 %psum.28 = f32[2,1792]{1,0:T(2,128)S(1)} all-reduce(f32[2,1792]{1,0:T(2,128)S(1)} %get-tuple-element.7), channel_id=1, replica_groups=mesh['row'=8,'col'=4] {'col'}, use_global_device_ids=true, to_apply=%region_1.0 | all-reduce | flops 3584 | bytes 28672 | tf_op jit(solution)/shard_map/psum | solution.py:21
  36.9 0.0 copy-done.3
  36.9 0.1 fusion.3
  37.0 0.0 copy-start.1
  37.0 22.3 %all-reduce = (f32[2]{0:T(128)S(1)}, f32[2,2048]{1,0:T(2,128)S(1)}) all-reduce(f32[2]{0:T(128)S(1)} %get-tuple-element.10, f32[2,2048]{1,0:T(2,128)S(1)} %get-tuple-element.6), channel_id=1, replica_groups=mesh['row'=8,'col'=4] {'row'}, use_global_device_ids=true, to_apply=%region_5.0 | all-reduce | flops 4098 | bytes 32784 | tf_op jit(solution)/shard_map/psum | solution.py:25
  59.4 0.0 copy-done.2
  59.4 0.0 copy-start
  59.4 11.5 %multiply_reduce_fusion = f32[2]{0:T(128)S(1)} fusion(f32[2]{0:T(128)S(1)} %broadcast_multiply_fusion, f32[2,2048]{1,0:T(2,128)S(1)} %add_multiply_fusion, f32[2,1792]{1,0:T(2,128)S(1)} %get-tuple-element.11, bf16[2,1792,2048]{2,1,0:T(8,128)(2,1)} %param.7), kind=kLoop, calls=%fused_computation.5 | loop fusion | flops 44040192 | bytes 14710800 | tf_op jit(solution)/shard_map/reduce_sum | solution.py:28
  70.9 0.0 all-gather.2.cloned.1.call-update
  71.0 0.0 reduce-scatter.2.cloned.1.call-start
  71.0 37.5 %psum.31 = f32[2]{0:T(128)S(1)} all-reduce(f32[2]{0:T(128)S(1)} %multiply_reduce_fusion), channel_id=1, replica_groups=mesh['row'=8,'col'=4] {'row','col'}, use_global_device_ids=true, to_apply=%region_7.0 | all-reduce | flops 2 | bytes 16 | tf_op jit(solution)/shard_map/psum | solution.py:28
  108.6 20.8 %subtract_convert_fusion = bf16[2,1792,2048]{2,1,0:T(8,128)(2,1)} fusion(bf16[2,1792,2048]{2,1,0:T(8,128)(2,1)} %param.6, f32[2]{0:T(128)S(1)} %sqrt_maximum_fusion, f32[2]{0:T(128)S(1)} %broadcast_multiply_fusion, f32[2,2048]{1,0:T(2,128)S(1)} %add_multiply_fusion, f32[2,1792]{1,0:T(2,128)S(1)} %get-tuple-element.11, bf16[2,1792,2048]{2,1,0:T(8,128)(2,1)} %param.7), kind=kLoop, calls=%fused_computation.4 | loop fusion | flops 66060288 | bytes 44070928 | tf_op jit(solution)/shard_map/convert_element_type | solution.py:32
  129.3 0.0 copy-done.1
  129.3 0.0 copy-done
  129.3 0.0 all-gather.2.cloned.1.call-done
  129.4 21.9 %convolution_bitcast_fusion = f32[1024,3584]{0,1:T(8,128)} fusion(bf16[3584,2048]{1,0:T(8,128)(2,1)} %bitcast.5, bf16[1024,2048]{1,0:T(8,128)(2,1)} %all-gather.2.cloned.1.call-done), kind=kOutput, calls=%fused_computation.6 | convolution fusion | flops 15032385536 | bytes 33554432 | tf_op jit(solution)/shard_map/dot_general | solution.py:36
  151.3 0.0 reduce-scatter.2.cloned.1.call-update
  151.3 247.1 %reduce-scatter.2.cloned.1.call-done = f32[256,3584]{0,1:T(8,128)} async-done(((f32[1024,3584]{0,1:T(8,128)}), f32[256,3584]{0,1:T(8,128)}) %reduce-scatter.2.cloned.1.call-update) | async-done | bytes 3670032 | tf_op jit(solution)/shard_map/reduce_scatter | solution.py:35
  398.4 2.6 fusion.2
  401.0 1.4 copy.8
  (3 shorter events, 0.0 us)
Async XLA Ops:
  7.2 29.7 %copy-start.3 = (f32[2,1792]{1,0:T(2,128)S(1)}, f32[2,1792]{1,0:T(2,128)}, u32[]{:S(2)}) copy-start(f32[2,1792]{1,0:T(2,128)} %param.8) | copy-start | bytes 43012
  7.2 52.2 %copy-start.2 = (f32[2,2048]{1,0:T(2,128)S(1)}, f32[2,2048]{1,0:T(2,128)}, u32[]{:S(2)}) copy-start(f32[2,2048]{1,0:T(2,128)} %param.9) | copy-start | bytes 49156
  7.2 122.2 %all-gather.2.cloned.1.call-start = ((), (), s32[]{:S(2)}) async-start(), calls=%async_computation.1 | async-start | bytes 4718592 | tf_op jit(solution)/shard_map/all_gather | solution.py:33
  37.0 92.3 %copy-start.1 = (f32[2,1792]{1,0:T(2,128)}, f32[2,1792]{1,0:T(2,128)S(1)}, u32[]{:S(2)}) copy-start(f32[2,1792]{1,0:T(2,128)S(1)} %get-tuple-element.11) | copy-start | bytes 43012
  59.4 69.9 %copy-start = (f32[2,2048]{1,0:T(2,128)}, f32[2,2048]{1,0:T(2,128)S(1)}, u32[]{:S(2)}) copy-start(f32[2,2048]{1,0:T(2,128)S(1)} %add_multiply_fusion) | copy-start | bytes 49156
  71.0 327.4 %reduce-scatter.2.cloned.1.call-start = ((), (), s32[]{:S(2)}) async-start(), calls=%async_computation.2 | async-start | bytes 18350080 | tf_op jit(solution)/shard_map/reduce_scatter | solution.py:35
Sparse Core Ops, SparseCore 0:
  71.1 34.2 all-gather.1
  151.4 246.9 reduce-scatter.1
where the time goes:
time: 410 us; the launch traced here: 409 us
  waiting for transfers between devices  247 us (60%)
  blocking collectives  80.4 us (20%)
  other arithmetic  44.1 us (11%)
  matrix products  21.9 us (5%)
  between operations  14.1 us (3%)
    reduce_scatter x1, waiting for transfers between devices, local(): lax.psum_scatter(lax.dot_general(spread, flat_weights, (((1,), (1,)), (()...  247 us
    psum x1, blocking collectives, local(): norm_total = lax.psum(jnp.sum(update * update, axis=(1, 2)), ('row', 'col'))  37.5 us
    psum x1, blocking collectives, local(): row_mean = lax.psum(jnp.sum(row_new, axis=1), 'row') / FF  22.3 us
    dot_general x1, matrix products, local(): lax.dot_general(spread, flat_weights, (((1,), (1,)), ((), ())), preferred...  21.9 us
    convert_element_type x1, other arithmetic, local(): new_weights = (weights.astype(jnp.float32) - learn_rate * update / clip_s...  20.8 us
    psum x1, blocking collectives, local(): row_total = lax.psum(row_part, 'col')  20.5 us
    reduce_sum x1, other arithmetic, local(): norm_total = lax.psum(jnp.sum(update * update, axis=(1, 2)), ('row', 'col'))  11.5 us
    reduce_sum x1, other arithmetic, local(): col_part = jnp.sum(squares, axis=1)  9.13 us
  transfers between devices with their start and end apart: 2, of which 1 were waited for; matrix products, arithmetic and copies ran while one was open for 5% of the time, Pallas kernels for 0%

commit v1 on v0

--- a/solution.py
+++ b/solution.py
@@ -25,7 +25,11 @@
     row_mean = lax.psum(jnp.sum(row_new, axis=1), "row") / FF
     denominator = jnp.sqrt(row_new[:, :, None] * col_new[:, None, :] / row_mean[:, None, None])
     update = gradient / denominator
-    norm_total = lax.psum(jnp.sum(update * update, axis=(1, 2)), ("row", "col"))
+
+    def group_inputs(local_x, row_axis, link_axis):
+        return jax.lax.psum(jax.lax.psum(local_x, row_axis), link_axis)
+
+    norm_total = group_inputs(jnp.sum(update * update, axis=(1, 2)), "row", link_axis="col")
     clip_scale = jnp.maximum(1.0, jnp.sqrt(norm_total / (FF * D)) / clip_limit)
     new_weights = (
         weights.astype(jnp.float32) - learn_rate * update / clip_scale[:, None, None]

time: 410 us -> 396 us (0.966)
  blocking collectives: 80.4 us -> 63.2 us
    psum x1 -> x2, blocking collectives: 37.5 us -> 20.3 us  [group_inputs(): return jax.lax.psum(jax.lax.psum(local_x, row_axis), link_axis)]
    all_gather x1, waiting for transfers between devices: 0.02 us -> 4.35 us  [local(): spread = lax.all_gather(tokens, 'row', axis=0, tiled=True)]
  transfers between devices with their start and end apart: 2 -> 2, of which waited for: 1 -> 2; matrix products, arithmetic and copies ran while one was open for 5% -> 5% of each run, Pallas kernels for 0% -> 0%
where the time goes in v1:
time: 396 us; the launch traced here: 395 us
  waiting for transfers between devices  250 us (63%)
  blocking collectives  63.2 us (16%)
  other arithmetic  44.4 us (11%)
  matrix products  21.9 us (6%)
  between operations  14.1 us (4%)
    reduce_scatter x1, waiting for transfers between devices, local(): lax.psum_scatter(lax.dot_general(spread, flat_weights, (((1,), (1,)), (()...  246 us
    psum x1, blocking collectives, local(): row_mean = lax.psum(jnp.sum(row_new, axis=1), 'row') / FF  22.3 us
    dot_general x1, matrix products, local(): lax.dot_general(spread, flat_weights, (((1,), (1,)), ((), ())), preferred...  21.9 us
    convert_element_type x1, other arithmetic, local(): new_weights = (weights.astype(jnp.float32) - learn_rate * update / clip_s...  21.1 us
    psum x1, blocking collectives, local(): row_total = lax.psum(row_part, 'col')  20.5 us
    psum x2, blocking collectives, group_inputs(): return jax.lax.psum(jax.lax.psum(local_x, row_axis), link_axis)  20.3 us
    reduce_sum x1, other arithmetic, local(): jnp.sum(update * update, axis=(1, 2))  11.5 us
    reduce_sum x1, other arithmetic, local(): col_part = jnp.sum(squares, axis=1)  9.13 us
  transfers between devices with their start and end apart: 2, of which 2 were waited for; matrix products, arithmetic and copies ran while one was open for 5% of the time, Pallas kernels for 0%

profile of v1, /device:TPU:0, one launch (start us, length us, event | category | flops | bytes accessed | tf_op | source)
XLA Modules:
  0.0 395.4 jit_solution(11339273190184058073)
XLA Ops:
  7.2 0.0 copy-start.3
  7.2 0.0 copy-start.2
  7.2 0.0 all-gather.2.cloned.1.call-start
  7.2 9.1 %fusion = (f32[2,2048]{1,0:T(2,128)S(1)}, f32[2,1792]{1,0:T(2,128)S(1)}) fusion(bf16[2,1792,2048]{2,1,0:T(8,128)(2,1)} %param.7), kind=kLoop, calls=%fused_computation.2 | loop fusion | flops 29352448 | bytes 14710784 | tf_op jit(solution)/shard_map/reduce_sum | solution.py:18
  16.4 20.5 %psum.35 = f32[2,1792]{1,0:T(2,128)S(1)} all-reduce(f32[2,1792]{1,0:T(2,128)S(1)} %get-tuple-element.7), channel_id=1, replica_groups=mesh['row'=8,'col'=4] {'col'}, use_global_device_ids=true, to_apply=%region_1.0 | all-reduce | flops 3584 | bytes 28672 | tf_op jit(solution)/shard_map/psum | solution.py:21
  36.9 0.0 copy-done.3
  36.9 0.1 fusion.3
  37.0 0.0 copy-start.1
  37.0 22.3 %all-reduce = (f32[2]{0:T(128)S(1)}, f32[2,2048]{1,0:T(2,128)S(1)}) all-reduce(f32[2]{0:T(128)S(1)} %get-tuple-element.10, f32[2,2048]{1,0:T(2,128)S(1)} %get-tuple-element.6), channel_id=1, replica_groups=mesh['row'=8,'col'=4] {'row'}, use_global_device_ids=true, to_apply=%region_5.0 | all-reduce | flops 4098 | bytes 32784 | tf_op jit(solution)/shard_map/psum | solution.py:25
  59.4 0.0 copy-done.2
  59.4 0.0 copy-start
  59.4 11.5 %multiply_reduce_fusion = f32[2]{0:T(128)S(1)} fusion(f32[2]{0:T(128)S(1)} %broadcast_multiply_fusion, f32[2,2048]{1,0:T(2,128)S(1)} %add_multiply_fusion, f32[2,1792]{1,0:T(2,128)S(1)} %get-tuple-element.11, bf16[2,1792,2048]{2,1,0:T(8,128)(2,1)} %param.7), kind=kLoop, calls=%fused_computation.5 | loop fusion | flops 44040192 | bytes 14710800 | tf_op jit(solution)/shard_map/reduce_sum | solution.py:32
  70.9 11.8 %psum.38 = f32[2]{0:T(128)S(1)} all-reduce(f32[2]{0:T(128)S(1)} %multiply_reduce_fusion), channel_id=1, replica_groups=mesh['row'=8,'col'=4] {'row'}, use_global_device_ids=true, to_apply=%region_7.0 | all-reduce | flops 2 | bytes 16 | tf_op jit(solution)/shard_map/psum | solution.py:30
  82.7 0.0 all-gather.2.cloned.1.call-update
  82.7 0.0 reduce-scatter.2.cloned.1.call-start
  82.8 8.6 %psum.39 = f32[2]{0:T(128)S(1)} all-reduce(f32[2]{0:T(128)S(1)} %psum.38), channel_id=1, replica_groups=mesh['row'=8,'col'=4] {'col'}, use_global_device_ids=true, to_apply=%region_8.0 | all-reduce | flops 2 | bytes 16 | tf_op jit(solution)/shard_map/psum | solution.py:30
  91.3 21.1 %subtract_convert_fusion = bf16[2,1792,2048]{2,1,0:T(8,128)(2,1)} fusion(bf16[2,1792,2048]{2,1,0:T(8,128)(2,1)} %param.6, f32[2]{0:T(128)S(1)} %sqrt_maximum_fusion, f32[2]{0:T(128)S(1)} %broadcast_multiply_fusion, f32[2,2048]{1,0:T(2,128)S(1)} %add_multiply_fusion, f32[2,1792]{1,0:T(2,128)S(1)} %get-tuple-element.11, bf16[2,1792,2048]{2,1,0:T(8,128)(2,1)} %param.7), kind=kLoop, calls=%fused_computation.4 | loop fusion | flops 66060288 | bytes 44070928 | tf_op jit(solution)/shard_map/convert_element_type | solution.py:36
  112.4 0.0 copy-done.1
  112.4 0.0 copy-done
  112.4 4.3 %all-gather.2.cloned.1.call-done = bf16[1024,2048]{1,0:T(8,128)(2,1)} async-done(((bf16[128,2048]{1,0:T(8,128)(2,1)}), bf16[1024,2048]{1,0:T(8,128)(2,1)}) %all-gather.2.cloned.1.call-update) | async-done | bytes 4194320 | tf_op jit(solution)/shard_map/all_gather | solution.py:37
  116.8 21.9 %convolution_bitcast_fusion = f32[1024,3584]{0,1:T(8,128)} fusion(bf16[3584,2048]{1,0:T(8,128)(2,1)} %bitcast.5, bf16[1024,2048]{1,0:T(8,128)(2,1)} %all-gather.2.cloned.1.call-done), kind=kOutput, calls=%fused_computation.6 | convolution fusion | flops 15032385536 | bytes 33554432 | tf_op jit(solution)/shard_map/dot_general | solution.py:40
  138.7 0.0 reduce-scatter.2.cloned.1.call-update
  138.7 245.9 %reduce-scatter.2.cloned.1.call-done = f32[256,3584]{0,1:T(8,128)} async-done(((f32[1024,3584]{0,1:T(8,128)}), f32[256,3584]{0,1:T(8,128)}) %reduce-scatter.2.cloned.1.call-update) | async-done | bytes 3670032 | tf_op jit(solution)/shard_map/reduce_scatter | solution.py:39
  384.6 2.6 fusion.2
  387.2 1.4 copy.8
  (3 shorter events, 0.0 us)
Async XLA Ops:
  7.2 29.7 %copy-start.3 = (f32[2,1792]{1,0:T(2,128)S(1)}, f32[2,1792]{1,0:T(2,128)}, u32[]{:S(2)}) copy-start(f32[2,1792]{1,0:T(2,128)} %param.8) | copy-start | bytes 43012
  7.2 52.2 %copy-start.2 = (f32[2,2048]{1,0:T(2,128)S(1)}, f32[2,2048]{1,0:T(2,128)}, u32[]{:S(2)}) copy-start(f32[2,2048]{1,0:T(2,128)} %param.9) | copy-start | bytes 49156
  7.2 109.6 %all-gather.2.cloned.1.call-start = ((), (), s32[]{:S(2)}) async-start(), calls=%async_computation.1 | async-start | bytes 4718592 | tf_op jit(solution)/shard_map/all_gather | solution.py:37
  37.0 75.4 %copy-start.1 = (f32[2,1792]{1,0:T(2,128)}, f32[2,1792]{1,0:T(2,128)S(1)}, u32[]{:S(2)}) copy-start(f32[2,1792]{1,0:T(2,128)S(1)} %get-tuple-element.11) | copy-start | bytes 43012
  59.4 53.0 %copy-start = (f32[2,2048]{1,0:T(2,128)}, f32[2,2048]{1,0:T(2,128)S(1)}, u32[]{:S(2)}) copy-start(f32[2,2048]{1,0:T(2,128)S(1)} %add_multiply_fusion) | copy-start | bytes 49156
  82.7 301.9 %reduce-scatter.2.cloned.1.call-start = ((), (), s32[]{:S(2)}) async-start(), calls=%async_computation.2 | async-start | bytes 18350080 | tf_op jit(solution)/shard_map/reduce_scatter | solution.py:39
Sparse Core Ops, SparseCore 0:
  82.8 33.8 all-gather.1
  138.8 245.7 reduce-scatter.1

commit v2 on v0

--- a/solution.py
+++ b/solution.py
@@ -1,3 +1,4 @@
+import functools
 import jax
 import jax.numpy as jnp
 from jax import lax
@@ -9,6 +10,13 @@
 learn_rate = 0.01
 clip_limit = 1.0
 tiny_eps = 1e-30
+
+
+def move_scenes_by_axis(row_data, axis_key):
+    return lax.all_gather(row_data, axis_key).sum(axis=0)
+
+
+tokens_compute = functools.partial(move_scenes_by_axis, axis_key=("row", "col"))
 
 
 def local(tokens, weights, gradients, row_factors, col_factors):
@@ -25,7 +33,7 @@
     row_mean = lax.psum(jnp.sum(row_new, axis=1), "row") / FF
     denominator = jnp.sqrt(row_new[:, :, None] * col_new[:, None, :] / row_mean[:, None, None])
     update = gradient / denominator
-    norm_total = lax.psum(jnp.sum(update * update, axis=(1, 2)), ("row", "col"))
+    norm_total = tokens_compute(jnp.sum(update * update, axis=(1, 2)))
     clip_scale = jnp.maximum(1.0, jnp.sqrt(norm_total / (FF * D)) / clip_limit)
     new_weights = (
         weights.astype(jnp.float32) - learn_rate * update / clip_scale[:, None, None]

time: 410 us -> 411 us (level)
    psum x1 -> x0, blocking collectives: 37.5 us -> none  [local(): norm_total = lax.psum(jnp.sum(update * update, axis=(1, 2)), ('row', 'col'))]
    unnamed x0 -> x1, blocking collectives: none -> 37.1 us
    reduce_sum x1 -> x2, other arithmetic: 11.5 us -> 11.5 us  [the longest x1 11.5 us: local(): norm_total = tokens_compute(jnp.sum(update * update, axis=(1, 2)))]
  transfers between devices with their start and end apart: 2 -> 2, of which waited for: 1 -> 1; matrix products, arithmetic and copies ran while one was open for 5% -> 10% of each run, Pallas kernels for 0% -> 0%
where the time goes in v2:
time: 411 us; the launch traced here: 410 us
  waiting for transfers between devices  248 us (60%)
  blocking collectives  80.5 us (20%)
  other arithmetic  44.2 us (11%)
  matrix products  21.9 us (5%)
  between operations  14.1 us (3%)
    reduce_scatter x1, waiting for transfers between devices, local(): lax.psum_scatter(lax.dot_general(spread, flat_weights, (((1,), (1,)), (()...  247 us
    unnamed x1, blocking collectives  37.1 us
    psum x1, blocking collectives, local(): row_mean = lax.psum(jnp.sum(row_new, axis=1), 'row') / FF  22.9 us
    dot_general x1, matrix products, local(): lax.dot_general(spread, flat_weights, (((1,), (1,)), ((), ())), preferred...  21.9 us
    convert_element_type x1, other arithmetic, local(): new_weights = (weights.astype(jnp.float32) - learn_rate * update / clip_s...  20.8 us
    psum x1, blocking collectives, local(): row_total = lax.psum(row_part, 'col')  20.5 us
    reduce_sum x1, other arithmetic, local(): norm_total = tokens_compute(jnp.sum(update * update, axis=(1, 2)))  11.5 us
    reduce_sum x1, other arithmetic, local(): col_part = jnp.sum(squares, axis=1)  9.13 us
  transfers between devices with their start and end apart: 2, of which 1 were waited for; matrix products, arithmetic and copies ran while one was open for 10% of the time, Pallas kernels for 0%

profile of v2, /device:TPU:0, one launch (start us, length us, event | category | flops | bytes accessed | tf_op | source)
XLA Modules:
  0.0 410.3 jit_solution(7428183282962463979)
XLA Ops:
  7.2 0.0 copy-start.3
  7.2 0.0 copy-start.2
  7.2 0.0 all-gather.3.cloned.1.call-start
  7.2 0.7 all-gather.3.cloned.1.call-update
  7.9 0.0 reduce-scatter.2.cloned.1.call-start
  8.0 9.1 %fusion = (f32[2,2048]{1,0:T(2,128)S(1)}, f32[2,1792]{1,0:T(2,128)S(1)}) fusion(bf16[2,1792,2048]{2,1,0:T(8,128)(2,1)} %param.7), kind=kLoop, calls=%fused_computation.2 | loop fusion | flops 29352448 | bytes 14710784 | tf_op jit(solution)/shard_map/reduce_sum | solution.py:26
  17.1 20.5 %psum.21 = f32[2,1792]{1,0:T(2,128)S(1)} all-reduce(f32[2,1792]{1,0:T(2,128)S(1)} %get-tuple-element.10), channel_id=1, replica_groups=mesh['row'=8,'col'=4] {'col'}, use_global_device_ids=true, to_apply=%region_1.0 | all-reduce | flops 3584 | bytes 28672 | tf_op jit(solution)/shard_map/psum | solution.py:29
  37.6 0.0 copy-done.3
  37.6 0.1 fusion.3
  37.8 0.0 copy-start.1
  37.8 22.9 %all-reduce.1 = (f32[2]{0:T(128)S(1)}, f32[2,2048]{1,0:T(2,128)S(1)}) all-reduce(f32[2]{0:T(128)S(1)} %get-tuple-element.13, f32[2,2048]{1,0:T(2,128)S(1)} %get-tuple-element.9), channel_id=1, replica_groups=mesh['row'=8,'col'=4] {'row'}, use_global_device_ids=true, to_apply=%region_5.0 | all-reduce | flops 4098 | bytes 32784 | tf_op jit(solution)/shard_map/psum | solution.py:33
  60.7 0.0 copy-done.2
  60.7 0.0 copy-start
  60.7 11.5 %multiply_reduce_fusion = f32[2]{0:T(128)S(1)} fusion(f32[2]{0:T(128)S(1)} %broadcast_multiply_fusion, f32[2,2048]{1,0:T(2,128)S(1)} %add_multiply_fusion, f32[2,1792]{1,0:T(2,128)S(1)} %get-tuple-element.14, bf16[2,1792,2048]{2,1,0:T(8,128)(2,1)} %param.7), kind=kLoop, calls=%fused_computation.5 | loop fusion | flops 44040192 | bytes 14710800 | tf_op jit(solution)/shard_map/reduce_sum | solution.py:36
  72.2 0.2 dynamic-update-slice
  72.4 37.1 %all-reduce = f32[64]{0:T(128)S(1)} all-reduce(f32[64]{0:T(128)S(1)} %dynamic-update-slice), channel_id=2, replica_groups=mesh['row'=8,'col'=4] {'row','col'}, use_global_device_ids=true, to_apply=%add | all-reduce | flops 64 | bytes 512
  109.5 0.1 reshape.18
  109.6 20.8 %subtract_convert_fusion = bf16[2,1792,2048]{2,1,0:T(8,128)(2,1)} fusion(bf16[2,1792,2048]{2,1,0:T(8,128)(2,1)} %param.6, f32[2]{0:T(128)S(1)} %sqrt_maximum_fusion, f32[2]{0:T(128)S(1)} %broadcast_multiply_fusion, f32[2,2048]{1,0:T(2,128)S(1)} %add_multiply_fusion, f32[2,1792]{1,0:T(2,128)S(1)} %get-tuple-element.14, bf16[2,1792,2048]{2,1,0:T(8,128)(2,1)} %param.7), kind=kLoop, calls=%fused_computation.4 | loop fusion | flops 66060288 | bytes 44070928 | tf_op jit(solution)/shard_map/convert_element_type | solution.py:40
  130.4 0.0 copy-done.1
  130.4 0.0 copy-done
  130.4 0.0 all-gather.3.cloned.1.call-done
  130.4 21.9 %convolution_bitcast_fusion = f32[1024,3584]{0,1:T(8,128)} fusion(bf16[3584,2048]{1,0:T(8,128)(2,1)} %bitcast.5, bf16[1024,2048]{1,0:T(8,128)(2,1)} %all-gather.3.cloned.1.call-done), kind=kOutput, calls=%fused_computation.6 | convolution fusion | flops 15032385536 | bytes 33554432 | tf_op jit(solution)/shard_map/dot_general | solution.py:44
  152.3 0.0 reduce-scatter.2.cloned.1.call-update
  152.3 247.2 %reduce-scatter.2.cloned.1.call-done = f32[256,3584]{0,1:T(8,128)} async-done(((f32[1024,3584]{0,1:T(8,128)}), f32[256,3584]{0,1:T(8,128)}) %reduce-scatter.2.cloned.1.call-update) | async-done | bytes 3670032 | tf_op jit(solution)/shard_map/reduce_scatter | solution.py:43
  399.5 2.6 fusion.2
  402.1 1.4 copy.9
  (5 shorter events, 0.1 us)
Async XLA Ops:
  7.2 30.5 %copy-start.3 = (f32[2,1792]{1,0:T(2,128)S(1)}, f32[2,1792]{1,0:T(2,128)}, u32[]{:S(2)}) copy-start(f32[2,1792]{1,0:T(2,128)} %param.8) | copy-start | bytes 43012
  7.2 53.5 %copy-start.2 = (f32[2,2048]{1,0:T(2,128)S(1)}, f32[2,2048]{1,0:T(2,128)}, u32[]{:S(2)}) copy-start(f32[2,2048]{1,0:T(2,128)} %param.9) | copy-start | bytes 49156
  7.2 123.2 %all-gather.3.cloned.1.call-start = ((), (), s32[]{:S(2)}) async-start(), calls=%async_computation.1 | async-start | bytes 4718592 | tf_op jit(solution)/shard_map/all_gather | solution.py:41
  7.9 391.6 %reduce-scatter.2.cloned.1.call-start = ((), (), s32[]{:S(2)}) async-start(), calls=%async_computation.2 | async-start | bytes 18350080 | tf_op jit(solution)/shard_map/reduce_scatter | solution.py:43
  37.8 92.6 %copy-start.1 = (f32[2,1792]{1,0:T(2,128)}, f32[2,1792]{1,0:T(2,128)S(1)}, u32[]{:S(2)}) copy-start(f32[2,1792]{1,0:T(2,128)S(1)} %get-tuple-element.14) | copy-start | bytes 43012
  60.7 69.7 %copy-start = (f32[2,2048]{1,0:T(2,128)}, f32[2,2048]{1,0:T(2,128)S(1)}, u32[]{:S(2)}) copy-start(f32[2,2048]{1,0:T(2,128)S(1)} %add_multiply_fusion) | copy-start | bytes 49156
Sparse Core Ops, SparseCore 0:
  9.9 39.3 all-gather.2
  152.5 247.0 reduce-scatter.1
